TPU v7x, 128 devices: a whole 4x4x4 slice. The times are simulated.
128 devices in a mesh: basin: 16 (over y, x), tile: 8 (over z, core).
Axes of the slice: x: 4, y: 4, z: 4, core: 2. Of those that a mesh axis runs over, the one named last changes fastest.
Arguments:
- tile_water: float32 [16, 128, 4096], P('basin', None, 'tile'), may hold values from 0.1 to 3
- tile_frac: float32 [16, 128, 4096], P('basin', None, 'tile'), may hold values from 0.01 to 0.12
- tile_cell: int32 [16, 128, 4096], P('basin', None, 'tile'), may hold values from 0 to 255
- storage: float32 [16, 128, 256], P('basin', 'tile'), may hold values from 0 to 2
- kappa: float32 [16, 128, 256], P('basin', 'tile'), may hold values from 0.4 to 1
- inverse: float32 [16, 128, 256, 256], P('basin', 'tile'), may hold values from -0.25 to 1.15
- cell_mask: int32 [16, 128, 256], P('basin', 'tile'), may hold values 0 or 1
- upstream: int32 [16, 128], P('basin', 'tile'), may hold values from 0 to 15, as said below
Outputs:
- level: float32 [16, 128, 256], P('basin', 'tile')
- discharge: float32 [16, 128, 256], P('basin', 'tile')
Inputs may be any that keep to these rules, and one draw needn't show every extreme that they name: `upstream`: for each reach position and each group of 16 consecutive chains, the values form a permutation of 0 to 15.
All inputs are finite; a program needn't handle non-finite values. No bound on the sum of `cell_mask` on one device may be relied on, other than what follows from the above.
Results may differ from a plain program's by a relative error of at most 0.0001.
Values sent between devices are 32-bit elements; how exact they have to be, the bound alone decides.
No kernel may reach another device: no remote copies, remote signals or barrier semaphores. Data moves between devices by JAX's collectives and lax.ppermute only.
A program may use at most 64 MiB of HBM per device.

v0:
```python
import math

import jax
import jax.numpy as jnp
from jax import lax
from jax.sharding import PartitionSpec as P

SUBSTEPS = 3


time_step = 0.5


def in_blocks(value, dim, devices):
    before, after = (value.shape[:dim], value.shape[dim + 1 :])
    return jnp.moveaxis(value.reshape(*before, devices, -1, *after), dim, 0)


def sent_and_summed(value, axis, dim):
    devices = lax.axis_size(axis)
    pieces = lax.all_to_all(in_blocks(value, dim, devices), axis, 0, 0, tiled=True)
    return jnp.sum(pieces, axis=0)


def passed_along(value, axis, steps):
    count = lax.axis_size(axis)
    initial, last = (max(0, -steps), min(count, count - steps))
    return lax.ppermute(value, axis, [(source, source + steps) for source in range(initial, last)])


def local(tile_water, tile_frac, tile_cell, storage, kappa, inverse, cell_mask, upstream):
    product = tile_frac[0] * tile_water[0]
    cells = tile_cell[0]
    rows = storage.shape[1]
    width = storage.shape[2]
    tiles = product.shape[1]
    cell_ids = jnp.arange(width, dtype=jnp.int32)
    count = rows * lax.axis_size("tile")
    values = product
    owners = cells
    group = math.gcd(count, 4)
    values = values.reshape(count // group, group, tiles)
    owners = owners.reshape(count // group, group, tiles)

    def one_group(items):
        vals, owns = items
        table = (owns[:, :, None] == cell_ids[None, None, :]).astype(jnp.float32)
        return jnp.einsum("ct,ctj->cj", vals, table, precision=lax.Precision.HIGHEST)

    summed = lax.map(one_group, (values, owners))
    runoff = sent_and_summed(summed.reshape(count, width), "tile", 0)
    forcing = time_step * runoff
    mask = cell_mask[0].astype(jnp.float32)
    rates = kappa[0]
    matrices = inverse[0]
    links = upstream[0]
    level = storage[0]
    count = lax.axis_size("basin")
    selector = (links[:, None] == jnp.arange(rows, dtype=jnp.int32)[None, :]).astype(jnp.float32)

    def update(current, inflow):
        vector = current + forcing + inflow
        wet = mask * jnp.einsum("cjk,ck->cj", matrices, vector, precision=lax.Precision.HIGHEST)
        outflow = rates * wet
        return (wet - outflow, outflow)

    def pass_down(outflow):
        received = passed_along(outflow, "basin", 1)
        return jnp.dot(selector, received, precision=lax.Precision.HIGHEST)

    empty = jnp.zeros((rows, width), jnp.float32)
    position = lax.axis_index("basin")

    def front(turn, carry):
        current, outflow_kept, inflow = carry
        section = turn - position
        active = (section >= 0) & (section < SUBSTEPS)
        new_level, outflow = update(current, inflow)
        current = jnp.where(active, new_level, current)
        outflow_kept = jnp.where(active, outflow, outflow_kept)
        return (current, outflow_kept, pass_down(outflow))

    level, discharge, _ = lax.fori_loop(0, count + SUBSTEPS - 1, front, (level, empty, empty))
    return (level[None], discharge[None])


def solution(mesh):
    placed = (
        P("basin", None, "tile"),
        P("basin", None, "tile"),
        P("basin", None, "tile"),
        P("basin", "tile", None),
        P("basin", "tile", None),
        P("basin", "tile", None, None),
        P("basin", "tile", None),
        P("basin", "tile"),
    )
    return jax.shard_map(
        local,
        mesh=mesh,
        in_specs=placed,
        out_specs=(P("basin", "tile", None), P("basin", "tile", None)),
        check_vma=False,
    )
```

profile of v0, /device:TPU:8, one launch (start us, length us, event | category | flops | bytes accessed | tf_op | source)
XLA Modules:
  0.0 287.8 jit_solution(3553125871230454904)
XLA Ops:
  2.9 26.1 %while.29 = (s32[]{:T(128)}, f32[32,4,256]{2,1,0:T(4,128)S(1)}, f32[32,4,512]{2,1,0:T(4,128)S(1)}, s32[32,4,512]{2,1,0:T(4,128)S(1)}, s32[]{:T(128)}) while((s32[]{:T(128)}, f32[32,4,256]{2,1,0:T(4,128)S(1)}, f32[32,4,512]{2,1,0:T(4,128)S(1)}, s32[32,4,512]{2,1,0:T(4,128)S(1)}, s32[]{:T(128)}) %tuple.55), condition=%wide.region_1.2_spmd.clone, body=%wide.region_0.1_spmd.clone.sunk | while | flops 6815746 | bytes 61513 | solution.py:50
  29.7 5.3 %all-to-all-start = ((f32[8,16,256]{2,1,0:T(8,128)}), f32[8,16,256]{2,1,0:T(8,128)S(1)}, u32[]{:S(2)}, u32[]{:S(2)}) async-start(f32[8,16,256]{2,1,0:T(8,128)} %reshape_reshape.3), calls=%async_computation | async-start | bytes 262144 | tf_op jit(solution)/shard_map/all_to_all | solution.py:21
  35.0 6.1 %all-to-all-done = f32[8,16,256]{2,1,0:T(8,128)S(1)} async-done(((f32[8,16,256]{2,1,0:T(8,128)}), f32[8,16,256]{2,1,0:T(8,128)S(1)}, u32[]{:S(2)}, u32[]{:S(2)}) %all-to-all-start) | async-done | bytes 131104 | tf_op jit(solution)/shard_map/all_to_all | solution.py:21
  41.2 246.0 %while.30 = (s32[]{:T(128)}, f32[16,256]{1,0:T(8,128)S(1)}, f32[16,256]{1,0:T(8,128)S(1)}, f32[16,256]{1,0:T(8,128)S(1)}, s32[]{:T(128)}, /*index=5*/f32[16,256]...) while((s32[]{:T(128)}, f32[16,256]{1,0:T(8,128)S(1)}, ...), condition=%wide.region_4.5_spmd.clone, body=%wide.region_3.4_spmd.clone.sunk | while | flops 13406727 | bytes 4571410 | solution.py:83
  41.2 5.7 %fusion.28 = f32[16,1,256]{2,1,0:T(1,128)S(1)} fusion(f32[16,256,256]{2,1,0:T(8,128)} %get-tuple-element.415, f32[16,256,1]{1,0,2:T(8,128)S(1)} %add_bitcast_fusion.2), kind=kOutput, calls=%fused_computation.11.clone.1 | convolution fusion | flops 12582912 | bytes 4227072 | tf_op jit(solution)/shard_map/while/body/eval_jaxpr/cjk,ck->cj/dot_general | solution.py:63
  46.9 3.4 %collective-permute-start = (f32[16,256]{1,0:T(8,128)S(1)}, f32[16,256]{1,0:T(8,128)S(1)}, u32[]{:S(2)}, u32[]{:S(2)}) collective-permute-start(f32[16,256]{1,0:T(8,128)S(1)} %get-tuple-element.366), channel_id=1, source_target_pairs={{0,8},{8,16},{16,24},{24,32},{32,40},{40,48},{48,56},{56,64},{64,7... | collective-permute-start | bytes 49160 | tf_op jit(solution)/shard_map/while/body/eval_jaxpr/ppermute | solution.py:28
  50.3 4.3 %collective-permute-done = f32[16,256]{1,0:T(8,128)S(1)} collective-permute-done((f32[16,256]{1,0:T(8,128)S(1)}, f32[16,256]{1,0:T(8,128)S(1)}, u32[]{:S(2)}, u32[]{:S(2)}) %collective-permute-start) | collective-permute-done | bytes 16416 | tf_op jit(solution)/shard_map/while/body/eval_jaxpr/ppermute | solution.py:28
  54.9 5.7 %fusion.28 = f32[16,1,256]{2,1,0:T(1,128)S(1)} fusion(f32[16,256,256]{2,1,0:T(8,128)} %get-tuple-element.415, f32[16,256,1]{1,0,2:T(8,128)S(1)} %add_bitcast_fusion.2), kind=kOutput, calls=%fused_computation.11.clone.1 | convolution fusion | flops 12582912 | bytes 4227072 | tf_op jit(solution)/shard_map/while/body/eval_jaxpr/cjk,ck->cj/dot_general | solution.py:63
  60.5 1.9 collective-permute-start
  62.5 5.8 %collective-permute-done = f32[16,256]{1,0:T(8,128)S(1)} collective-permute-done((f32[16,256]{1,0:T(8,128)S(1)}, f32[16,256]{1,0:T(8,128)S(1)}, u32[]{:S(2)}, u32[]{:S(2)}) %collective-permute-start) | collective-permute-done | bytes 16416 | tf_op jit(solution)/shard_map/while/body/eval_jaxpr/ppermute | solution.py:28
  68.5 5.7 %fusion.28 = f32[16,1,256]{2,1,0:T(1,128)S(1)} fusion(f32[16,256,256]{2,1,0:T(8,128)} %get-tuple-element.415, f32[16,256,1]{1,0,2:T(8,128)S(1)} %add_bitcast_fusion.2), kind=kOutput, calls=%fused_computation.11.clone.1 | convolution fusion | flops 12582912 | bytes 4227072 | tf_op jit(solution)/shard_map/while/body/eval_jaxpr/cjk,ck->cj/dot_general | solution.py:63
  74.2 1.9 collective-permute-start
  76.2 5.8 %collective-permute-done = f32[16,256]{1,0:T(8,128)S(1)} collective-permute-done((f32[16,256]{1,0:T(8,128)S(1)}, f32[16,256]{1,0:T(8,128)S(1)}, u32[]{:S(2)}, u32[]{:S(2)}) %collective-permute-start) | collective-permute-done | bytes 16416 | tf_op jit(solution)/shard_map/while/body/eval_jaxpr/ppermute | solution.py:28
  82.2 5.7 %fusion.28 = f32[16,1,256]{2,1,0:T(1,128)S(1)} fusion(f32[16,256,256]{2,1,0:T(8,128)} %get-tuple-element.415, f32[16,256,1]{1,0,2:T(8,128)S(1)} %add_bitcast_fusion.2), kind=kOutput, calls=%fused_computation.11.clone.1 | convolution fusion | flops 12582912 | bytes 4227072 | tf_op jit(solution)/shard_map/while/body/eval_jaxpr/cjk,ck->cj/dot_general | solution.py:63
  89.8 5.8 %collective-permute-done = f32[16,256]{1,0:T(8,128)S(1)} collective-permute-done((f32[16,256]{1,0:T(8,128)S(1)}, f32[16,256]{1,0:T(8,128)S(1)}, u32[]{:S(2)}, u32[]{:S(2)}) %collective-permute-start) | collective-permute-done | bytes 16416 | tf_op jit(solution)/shard_map/while/body/eval_jaxpr/ppermute | solution.py:28
  95.9 5.7 %fusion.28 = f32[16,1,256]{2,1,0:T(1,128)S(1)} fusion(f32[16,256,256]{2,1,0:T(8,128)} %get-tuple-element.415, f32[16,256,1]{1,0,2:T(8,128)S(1)} %add_bitcast_fusion.2), kind=kOutput, calls=%fused_computation.11.clone.1 | convolution fusion | flops 12582912 | bytes 4227072 | tf_op jit(solution)/shard_map/while/body/eval_jaxpr/cjk,ck->cj/dot_general | solution.py:63
  103.5 5.8 %collective-permute-done = f32[16,256]{1,0:T(8,128)S(1)} collective-permute-done((f32[16,256]{1,0:T(8,128)S(1)}, f32[16,256]{1,0:T(8,128)S(1)}, u32[]{:S(2)}, u32[]{:S(2)}) %collective-permute-start) | collective-permute-done | bytes 16416 | tf_op jit(solution)/shard_map/while/body/eval_jaxpr/ppermute | solution.py:28
  109.5 5.7 %fusion.28 = f32[16,1,256]{2,1,0:T(1,128)S(1)} fusion(f32[16,256,256]{2,1,0:T(8,128)} %get-tuple-element.415, f32[16,256,1]{1,0,2:T(8,128)S(1)} %add_bitcast_fusion.2), kind=kOutput, calls=%fused_computation.11.clone.1 | convolution fusion | flops 12582912 | bytes 4227072 | tf_op jit(solution)/shard_map/while/body/eval_jaxpr/cjk,ck->cj/dot_general | solution.py:63
  117.2 5.8 %collective-permute-done = f32[16,256]{1,0:T(8,128)S(1)} collective-permute-done((f32[16,256]{1,0:T(8,128)S(1)}, f32[16,256]{1,0:T(8,128)S(1)}, u32[]{:S(2)}, u32[]{:S(2)}) %collective-permute-start) | collective-permute-done | bytes 16416 | tf_op jit(solution)/shard_map/while/body/eval_jaxpr/ppermute | solution.py:28
  123.2 5.7 %fusion.28 = f32[16,1,256]{2,1,0:T(1,128)S(1)} fusion(f32[16,256,256]{2,1,0:T(8,128)} %get-tuple-element.415, f32[16,256,1]{1,0,2:T(8,128)S(1)} %add_bitcast_fusion.2), kind=kOutput, calls=%fused_computation.11.clone.1 | convolution fusion | flops 12582912 | bytes 4227072 | tf_op jit(solution)/shard_map/while/body/eval_jaxpr/cjk,ck->cj/dot_general | solution.py:63
  130.8 5.8 %collective-permute-done = f32[16,256]{1,0:T(8,128)S(1)} collective-permute-done((f32[16,256]{1,0:T(8,128)S(1)}, f32[16,256]{1,0:T(8,128)S(1)}, u32[]{:S(2)}, u32[]{:S(2)}) %collective-permute-start) | collective-permute-done | bytes 16416 | tf_op jit(solution)/shard_map/while/body/eval_jaxpr/ppermute | solution.py:28
  136.9 5.7 %fusion.28 = f32[16,1,256]{2,1,0:T(1,128)S(1)} fusion(f32[16,256,256]{2,1,0:T(8,128)} %get-tuple-element.415, f32[16,256,1]{1,0,2:T(8,128)S(1)} %add_bitcast_fusion.2), kind=kOutput, calls=%fused_computation.11.clone.1 | convolution fusion | flops 12582912 | bytes 4227072 | tf_op jit(solution)/shard_map/while/body/eval_jaxpr/cjk,ck->cj/dot_general | solution.py:63
  144.5 5.8 %collective-permute-done = f32[16,256]{1,0:T(8,128)S(1)} collective-permute-done((f32[16,256]{1,0:T(8,128)S(1)}, f32[16,256]{1,0:T(8,128)S(1)}, u32[]{:S(2)}, u32[]{:S(2)}) %collective-permute-start) | collective-permute-done | bytes 16416 | tf_op jit(solution)/shard_map/while/body/eval_jaxpr/ppermute | solution.py:28
  150.5 5.7 %fusion.28 = f32[16,1,256]{2,1,0:T(1,128)S(1)} fusion(f32[16,256,256]{2,1,0:T(8,128)} %get-tuple-element.415, f32[16,256,1]{1,0,2:T(8,128)S(1)} %add_bitcast_fusion.2), kind=kOutput, calls=%fused_computation.11.clone.1 | convolution fusion | flops 12582912 | bytes 4227072 | tf_op jit(solution)/shard_map/while/body/eval_jaxpr/cjk,ck->cj/dot_general | solution.py:63
  158.2 5.8 %collective-permute-done = f32[16,256]{1,0:T(8,128)S(1)} collective-permute-done((f32[16,256]{1,0:T(8,128)S(1)}, f32[16,256]{1,0:T(8,128)S(1)}, u32[]{:S(2)}, u32[]{:S(2)}) %collective-permute-start) | collective-permute-done | bytes 16416 | tf_op jit(solution)/shard_map/while/body/eval_jaxpr/ppermute | solution.py:28
  164.2 5.7 %fusion.28 = f32[16,1,256]{2,1,0:T(1,128)S(1)} fusion(f32[16,256,256]{2,1,0:T(8,128)} %get-tuple-element.415, f32[16,256,1]{1,0,2:T(8,128)S(1)} %add_bitcast_fusion.2), kind=kOutput, calls=%fused_computation.11.clone.1 | convolution fusion | flops 12582912 | bytes 4227072 | tf_op jit(solution)/shard_map/while/body/eval_jaxpr/cjk,ck->cj/dot_general | solution.py:63
  171.8 5.8 %collective-permute-done = f32[16,256]{1,0:T(8,128)S(1)} collective-permute-done((f32[16,256]{1,0:T(8,128)S(1)}, f32[16,256]{1,0:T(8,128)S(1)}, u32[]{:S(2)}, u32[]{:S(2)}) %collective-permute-start) | collective-permute-done | bytes 16416 | tf_op jit(solution)/shard_map/while/body/eval_jaxpr/ppermute | solution.py:28
  177.9 5.7 %fusion.28 = f32[16,1,256]{2,1,0:T(1,128)S(1)} fusion(f32[16,256,256]{2,1,0:T(8,128)} %get-tuple-element.415, f32[16,256,1]{1,0,2:T(8,128)S(1)} %add_bitcast_fusion.2), kind=kOutput, calls=%fused_computation.11.clone.1 | convolution fusion | flops 12582912 | bytes 4227072 | tf_op jit(solution)/shard_map/while/body/eval_jaxpr/cjk,ck->cj/dot_general | solution.py:63
  185.5 5.8 %collective-permute-done = f32[16,256]{1,0:T(8,128)S(1)} collective-permute-done((f32[16,256]{1,0:T(8,128)S(1)}, f32[16,256]{1,0:T(8,128)S(1)}, u32[]{:S(2)}, u32[]{:S(2)}) %collective-permute-start) | collective-permute-done | bytes 16416 | tf_op jit(solution)/shard_map/while/body/eval_jaxpr/ppermute | solution.py:28
  191.5 5.7 %fusion.28 = f32[16,1,256]{2,1,0:T(1,128)S(1)} fusion(f32[16,256,256]{2,1,0:T(8,128)} %get-tuple-element.415, f32[16,256,1]{1,0,2:T(8,128)S(1)} %add_bitcast_fusion.2), kind=kOutput, calls=%fused_computation.11.clone.1 | convolution fusion | flops 12582912 | bytes 4227072 | tf_op jit(solution)/shard_map/while/body/eval_jaxpr/cjk,ck->cj/dot_general | solution.py:63
  199.2 5.8 %collective-permute-done = f32[16,256]{1,0:T(8,128)S(1)} collective-permute-done((f32[16,256]{1,0:T(8,128)S(1)}, f32[16,256]{1,0:T(8,128)S(1)}, u32[]{:S(2)}, u32[]{:S(2)}) %collective-permute-start) | collective-permute-done | bytes 16416 | tf_op jit(solution)/shard_map/while/body/eval_jaxpr/ppermute | solution.py:28
  205.2 5.7 %fusion.28 = f32[16,1,256]{2,1,0:T(1,128)S(1)} fusion(f32[16,256,256]{2,1,0:T(8,128)} %get-tuple-element.415, f32[16,256,1]{1,0,2:T(8,128)S(1)} %add_bitcast_fusion.2), kind=kOutput, calls=%fused_computation.11.clone.1 | convolution fusion | flops 12582912 | bytes 4227072 | tf_op jit(solution)/shard_map/while/body/eval_jaxpr/cjk,ck->cj/dot_general | solution.py:63
  212.8 5.8 %collective-permute-done = f32[16,256]{1,0:T(8,128)S(1)} collective-permute-done((f32[16,256]{1,0:T(8,128)S(1)}, f32[16,256]{1,0:T(8,128)S(1)}, u32[]{:S(2)}, u32[]{:S(2)}) %collective-permute-start) | collective-permute-done | bytes 16416 | tf_op jit(solution)/shard_map/while/body/eval_jaxpr/ppermute | solution.py:28
  218.9 5.7 %fusion.28 = f32[16,1,256]{2,1,0:T(1,128)S(1)} fusion(f32[16,256,256]{2,1,0:T(8,128)} %get-tuple-element.415, f32[16,256,1]{1,0,2:T(8,128)S(1)} %add_bitcast_fusion.2), kind=kOutput, calls=%fused_computation.11.clone.1 | convolution fusion | flops 12582912 | bytes 4227072 | tf_op jit(solution)/shard_map/while/body/eval_jaxpr/cjk,ck->cj/dot_general | solution.py:63
  224.6 1.9 collective-permute-start
  226.5 5.8 %collective-permute-done = f32[16,256]{1,0:T(8,128)S(1)} collective-permute-done((f32[16,256]{1,0:T(8,128)S(1)}, f32[16,256]{1,0:T(8,128)S(1)}, u32[]{:S(2)}, u32[]{:S(2)}) %collective-permute-start) | collective-permute-done | bytes 16416 | tf_op jit(solution)/shard_map/while/body/eval_jaxpr/ppermute | solution.py:28
  232.6 5.7 %fusion.28 = f32[16,1,256]{2,1,0:T(1,128)S(1)} fusion(f32[16,256,256]{2,1,0:T(8,128)} %get-tuple-element.415, f32[16,256,1]{1,0,2:T(8,128)S(1)} %add_bitcast_fusion.2), kind=kOutput, calls=%fused_computation.11.clone.1 | convolution fusion | flops 12582912 | bytes 4227072 | tf_op jit(solution)/shard_map/while/body/eval_jaxpr/cjk,ck->cj/dot_general | solution.py:63
  238.2 1.9 collective-permute-start
  240.2 5.8 %collective-permute-done = f32[16,256]{1,0:T(8,128)S(1)} collective-permute-done((f32[16,256]{1,0:T(8,128)S(1)}, f32[16,256]{1,0:T(8,128)S(1)}, u32[]{:S(2)}, u32[]{:S(2)}) %collective-permute-start) | collective-permute-done | bytes 16416 | tf_op jit(solution)/shard_map/while/body/eval_jaxpr/ppermute | solution.py:28
  246.2 5.7 %fusion.28 = f32[16,1,256]{2,1,0:T(1,128)S(1)} fusion(f32[16,256,256]{2,1,0:T(8,128)} %get-tuple-element.415, f32[16,256,1]{1,0,2:T(8,128)S(1)} %add_bitcast_fusion.2), kind=kOutput, calls=%fused_computation.11.clone.1 | convolution fusion | flops 12582912 | bytes 4227072 | tf_op jit(solution)/shard_map/while/body/eval_jaxpr/cjk,ck->cj/dot_general | solution.py:63
  251.9 1.9 collective-permute-start
  253.8 5.8 %collective-permute-done = f32[16,256]{1,0:T(8,128)S(1)} collective-permute-done((f32[16,256]{1,0:T(8,128)S(1)}, f32[16,256]{1,0:T(8,128)S(1)}, u32[]{:S(2)}, u32[]{:S(2)}) %collective-permute-start) | collective-permute-done | bytes 16416 | tf_op jit(solution)/shard_map/while/body/eval_jaxpr/ppermute | solution.py:28
  259.9 5.7 %fusion.28 = f32[16,1,256]{2,1,0:T(1,128)S(1)} fusion(f32[16,256,256]{2,1,0:T(8,128)} %get-tuple-element.415, f32[16,256,1]{1,0,2:T(8,128)S(1)} %add_bitcast_fusion.2), kind=kOutput, calls=%fused_computation.11.clone.1 | convolution fusion | flops 12582912 | bytes 4227072 | tf_op jit(solution)/shard_map/while/body/eval_jaxpr/cjk,ck->cj/dot_general | solution.py:63
  265.6 1.9 collective-permute-start
  267.5 5.8 %collective-permute-done = f32[16,256]{1,0:T(8,128)S(1)} collective-permute-done((f32[16,256]{1,0:T(8,128)S(1)}, f32[16,256]{1,0:T(8,128)S(1)}, u32[]{:S(2)}, u32[]{:S(2)}) %collective-permute-start) | collective-permute-done | bytes 16416 | tf_op jit(solution)/shard_map/while/body/eval_jaxpr/ppermute | solution.py:28
  273.6 5.7 %fusion.28 = f32[16,1,256]{2,1,0:T(1,128)S(1)} fusion(f32[16,256,256]{2,1,0:T(8,128)} %get-tuple-element.415, f32[16,256,1]{1,0,2:T(8,128)S(1)} %add_bitcast_fusion.2), kind=kOutput, calls=%fused_computation.11.clone.1 | convolution fusion | flops 12582912 | bytes 4227072 | tf_op jit(solution)/shard_map/while/body/eval_jaxpr/cjk,ck->cj/dot_general | solution.py:63
  279.2 1.9 collective-permute-start
  281.2 5.8 %collective-permute-done = f32[16,256]{1,0:T(8,128)S(1)} collective-permute-done((f32[16,256]{1,0:T(8,128)S(1)}, f32[16,256]{1,0:T(8,128)S(1)}, u32[]{:S(2)}, u32[]{:S(2)}) %collective-permute-start) | collective-permute-done | bytes 16416 | tf_op jit(solution)/shard_map/while/body/eval_jaxpr/ppermute | solution.py:28
  (232 shorter events, 52.8 us)
Async XLA Ops:
  0.6 40.5 %copy-start.1 = (f32[1,16,256]{2,1,0:T(8,128)S(1)}, f32[1,16,256]{2,1,0:T(8,128)}, u32[]{:S(2)}) copy-start(f32[1,16,256]{2,1,0:T(8,128)} %param.15) | copy-start | bytes 49156
  0.6 40.5 %copy-start.2 = (f32[1,16,256]{2,1,0:T(8,128)S(1)}, f32[1,16,256]{2,1,0:T(8,128)}, u32[]{:S(2)}) copy-start(f32[1,16,256]{2,1,0:T(8,128)} %param.16) | copy-start | bytes 49156
  0.7 34.3 %copy-start.4 = (s32[1,16,256]{2,1,0:T(8,128)S(1)}, s32[1,16,256]{2,1,0:T(8,128)}, u32[]{:S(2)}) copy-start(s32[1,16,256]{2,1,0:T(8,128)} %param.18) | copy-start | bytes 49156
  0.7 40.5 %copy-start.5 = (s32[1,16]{1,0:T(1,128)S(1)}, s32[1,16]{1,0:T(1,128)}, u32[]{:S(2)}) copy-start(s32[1,16]{1,0:T(1,128)} %param.19) | copy-start | bytes 196
  29.7 11.4 %all-to-all-start = ((f32[8,16,256]{2,1,0:T(8,128)}), f32[8,16,256]{2,1,0:T(8,128)S(1)}, u32[]{:S(2)}, u32[]{:S(2)}) async-start(f32[8,16,256]{2,1,0:T(8,128)} %reshape_reshape.3), calls=%async_computation | async-start | bytes 262144 | tf_op jit(solution)/shard_map/all_to_all | solution.py:21
  46.9 7.7 %collective-permute-start = (f32[16,256]{1,0:T(8,128)S(1)}, f32[16,256]{1,0:T(8,128)S(1)}, u32[]{:S(2)}, u32[]{:S(2)}) collective-permute-start(f32[16,256]{1,0:T(8,128)S(1)} %get-tuple-element.366), channel_id=1, source_target_pairs={{0,8},{8,16},{16,24},{24,32},{32,40},{40,48},{48,56},{56,64},{64,7... | collective-permute-start | bytes 49160 | tf_op jit(solution)/shard_map/while/body/eval_jaxpr/ppermute | solution.py:28
  60.5 7.7 %collective-permute-start = (f32[16,256]{1,0:T(8,128)S(1)}, f32[16,256]{1,0:T(8,128)S(1)}, u32[]{:S(2)}, u32[]{:S(2)}) collective-permute-start(f32[16,256]{1,0:T(8,128)S(1)} %get-tuple-element.366), channel_id=1, source_target_pairs={{0,8},{8,16},{16,24},{24,32},{32,40},{40,48},{48,56},{56,64},{64,7... | collective-permute-start | bytes 49160 | tf_op jit(solution)/shard_map/while/body/eval_jaxpr/ppermute | solution.py:28
  74.2 7.7 %collective-permute-start = (f32[16,256]{1,0:T(8,128)S(1)}, f32[16,256]{1,0:T(8,128)S(1)}, u32[]{:S(2)}, u32[]{:S(2)}) collective-permute-start(f32[16,256]{1,0:T(8,128)S(1)} %get-tuple-element.366), channel_id=1, source_target_pairs={{0,8},{8,16},{16,24},{24,32},{32,40},{40,48},{48,56},{56,64},{64,7... | collective-permute-start | bytes 49160 | tf_op jit(solution)/shard_map/while/body/eval_jaxpr/ppermute | solution.py:28
  87.9 7.7 %collective-permute-start = (f32[16,256]{1,0:T(8,128)S(1)}, f32[16,256]{1,0:T(8,128)S(1)}, u32[]{:S(2)}, u32[]{:S(2)}) collective-permute-start(f32[16,256]{1,0:T(8,128)S(1)} %get-tuple-element.366), channel_id=1, source_target_pairs={{0,8},{8,16},{16,24},{24,32},{32,40},{40,48},{48,56},{56,64},{64,7... | collective-permute-start | bytes 49160 | tf_op jit(solution)/shard_map/while/body/eval_jaxpr/ppermute | solution.py:28
  101.5 7.7 %collective-permute-start = (f32[16,256]{1,0:T(8,128)S(1)}, f32[16,256]{1,0:T(8,128)S(1)}, u32[]{:S(2)}, u32[]{:S(2)}) collective-permute-start(f32[16,256]{1,0:T(8,128)S(1)} %get-tuple-element.366), channel_id=1, source_target_pairs={{0,8},{8,16},{16,24},{24,32},{32,40},{40,48},{48,56},{56,64},{64,7... | collective-permute-start | bytes 49160 | tf_op jit(solution)/shard_map/while/body/eval_jaxpr/ppermute | solution.py:28
  115.2 7.7 %collective-permute-start = (f32[16,256]{1,0:T(8,128)S(1)}, f32[16,256]{1,0:T(8,128)S(1)}, u32[]{:S(2)}, u32[]{:S(2)}) collective-permute-start(f32[16,256]{1,0:T(8,128)S(1)} %get-tuple-element.366), channel_id=1, source_target_pairs={{0,8},{8,16},{16,24},{24,32},{32,40},{40,48},{48,56},{56,64},{64,7... | collective-permute-start | bytes 49160 | tf_op jit(solution)/shard_map/while/body/eval_jaxpr/ppermute | solution.py:28
  128.9 7.7 %collective-permute-start = (f32[16,256]{1,0:T(8,128)S(1)}, f32[16,256]{1,0:T(8,128)S(1)}, u32[]{:S(2)}, u32[]{:S(2)}) collective-permute-start(f32[16,256]{1,0:T(8,128)S(1)} %get-tuple-element.366), channel_id=1, source_target_pairs={{0,8},{8,16},{16,24},{24,32},{32,40},{40,48},{48,56},{56,64},{64,7... | collective-permute-start | bytes 49160 | tf_op jit(solution)/shard_map/while/body/eval_jaxpr/ppermute | solution.py:28
  142.6 7.7 %collective-permute-start = (f32[16,256]{1,0:T(8,128)S(1)}, f32[16,256]{1,0:T(8,128)S(1)}, u32[]{:S(2)}, u32[]{:S(2)}) collective-permute-start(f32[16,256]{1,0:T(8,128)S(1)} %get-tuple-element.366), channel_id=1, source_target_pairs={{0,8},{8,16},{16,24},{24,32},{32,40},{40,48},{48,56},{56,64},{64,7... | collective-permute-start | bytes 49160 | tf_op jit(solution)/shard_map/while/body/eval_jaxpr/ppermute | solution.py:28
  156.2 7.7 %collective-permute-start = (f32[16,256]{1,0:T(8,128)S(1)}, f32[16,256]{1,0:T(8,128)S(1)}, u32[]{:S(2)}, u32[]{:S(2)}) collective-permute-start(f32[16,256]{1,0:T(8,128)S(1)} %get-tuple-element.366), channel_id=1, source_target_pairs={{0,8},{8,16},{16,24},{24,32},{32,40},{40,48},{48,56},{56,64},{64,7... | collective-permute-start | bytes 49160 | tf_op jit(solution)/shard_map/while/body/eval_jaxpr/ppermute | solution.py:28
  169.9 7.7 %collective-permute-start = (f32[16,256]{1,0:T(8,128)S(1)}, f32[16,256]{1,0:T(8,128)S(1)}, u32[]{:S(2)}, u32[]{:S(2)}) collective-permute-start(f32[16,256]{1,0:T(8,128)S(1)} %get-tuple-element.366), channel_id=1, source_target_pairs={{0,8},{8,16},{16,24},{24,32},{32,40},{40,48},{48,56},{56,64},{64,7... | collective-permute-start | bytes 49160 | tf_op jit(solution)/shard_map/while/body/eval_jaxpr/ppermute | solution.py:28
  183.6 7.7 %collective-permute-start = (f32[16,256]{1,0:T(8,128)S(1)}, f32[16,256]{1,0:T(8,128)S(1)}, u32[]{:S(2)}, u32[]{:S(2)}) collective-permute-start(f32[16,256]{1,0:T(8,128)S(1)} %get-tuple-element.366), channel_id=1, source_target_pairs={{0,8},{8,16},{16,24},{24,32},{32,40},{40,48},{48,56},{56,64},{64,7... | collective-permute-start | bytes 49160 | tf_op jit(solution)/shard_map/while/body/eval_jaxpr/ppermute | solution.py:28
  197.2 7.7 %collective-permute-start = (f32[16,256]{1,0:T(8,128)S(1)}, f32[16,256]{1,0:T(8,128)S(1)}, u32[]{:S(2)}, u32[]{:S(2)}) collective-permute-start(f32[16,256]{1,0:T(8,128)S(1)} %get-tuple-element.366), channel_id=1, source_target_pairs={{0,8},{8,16},{16,24},{24,32},{32,40},{40,48},{48,56},{56,64},{64,7... | collective-permute-start | bytes 49160 | tf_op jit(solution)/shard_map/while/body/eval_jaxpr/ppermute | solution.py:28
  210.9 7.7 %collective-permute-start = (f32[16,256]{1,0:T(8,128)S(1)}, f32[16,256]{1,0:T(8,128)S(1)}, u32[]{:S(2)}, u32[]{:S(2)}) collective-permute-start(f32[16,256]{1,0:T(8,128)S(1)} %get-tuple-element.366), channel_id=1, source_target_pairs={{0,8},{8,16},{16,24},{24,32},{32,40},{40,48},{48,56},{56,64},{64,7... | collective-permute-start | bytes 49160 | tf_op jit(solution)/shard_map/while/body/eval_jaxpr/ppermute | solution.py:28
  224.6 7.7 %collective-permute-start = (f32[16,256]{1,0:T(8,128)S(1)}, f32[16,256]{1,0:T(8,128)S(1)}, u32[]{:S(2)}, u32[]{:S(2)}) collective-permute-start(f32[16,256]{1,0:T(8,128)S(1)} %get-tuple-element.366), channel_id=1, source_target_pairs={{0,8},{8,16},{16,24},{24,32},{32,40},{40,48},{48,56},{56,64},{64,7... | collective-permute-start | bytes 49160 | tf_op jit(solution)/shard_map/while/body/eval_jaxpr/ppermute | solution.py:28
  238.2 7.7 %collective-permute-start = (f32[16,256]{1,0:T(8,128)S(1)}, f32[16,256]{1,0:T(8,128)S(1)}, u32[]{:S(2)}, u32[]{:S(2)}) collective-permute-start(f32[16,256]{1,0:T(8,128)S(1)} %get-tuple-element.366), channel_id=1, source_target_pairs={{0,8},{8,16},{16,24},{24,32},{32,40},{40,48},{48,56},{56,64},{64,7... | collective-permute-start | bytes 49160 | tf_op jit(solution)/shard_map/while/body/eval_jaxpr/ppermute | solution.py:28
  251.9 7.7 %collective-permute-start = (f32[16,256]{1,0:T(8,128)S(1)}, f32[16,256]{1,0:T(8,128)S(1)}, u32[]{:S(2)}, u32[]{:S(2)}) collective-permute-start(f32[16,256]{1,0:T(8,128)S(1)} %get-tuple-element.366), channel_id=1, source_target_pairs={{0,8},{8,16},{16,24},{24,32},{32,40},{40,48},{48,56},{56,64},{64,7... | collective-permute-start | bytes 49160 | tf_op jit(solution)/shard_map/while/body/eval_jaxpr/ppermute | solution.py:28
  265.6 7.7 %collective-permute-start = (f32[16,256]{1,0:T(8,128)S(1)}, f32[16,256]{1,0:T(8,128)S(1)}, u32[]{:S(2)}, u32[]{:S(2)}) collective-permute-start(f32[16,256]{1,0:T(8,128)S(1)} %get-tuple-element.366), channel_id=1, source_target_pairs={{0,8},{8,16},{16,24},{24,32},{32,40},{40,48},{48,56},{56,64},{64,7... | collective-permute-start | bytes 49160 | tf_op jit(solution)/shard_map/while/body/eval_jaxpr/ppermute | solution.py:28
  279.2 7.7 %collective-permute-start = (f32[16,256]{1,0:T(8,128)S(1)}, f32[16,256]{1,0:T(8,128)S(1)}, u32[]{:S(2)}, u32[]{:S(2)}) collective-permute-start(f32[16,256]{1,0:T(8,128)S(1)} %get-tuple-element.366), channel_id=1, source_target_pairs={{0,8},{8,16},{16,24},{24,32},{32,40},{40,48},{48,56},{56,64},{64,7... | collective-permute-start | bytes 49160 | tf_op jit(solution)/shard_map/while/body/eval_jaxpr/ppermute | solution.py:28
  287.2 0.6 copy-start
  287.2 0.6 copy-start.3
where the time goes:
time: 289 us; the launch traced here: 288 us
  matrix products  131 us (45%)
  waiting for transfers between devices  109 us (38%)
  starting transfers between devices  41.4 us (14%)
  local copies, waits for them, and re-layouts  2.9 us (1%)
    ppermute x18, waiting for transfers between devices, passed_along(): lax.ppermute(value, axis, [(source, source + steps) for source in range(i...  103 us
    dot_general x18, matrix products, update(): jnp.einsum('cjk,ck->cj', matrices, vector, precision=lax.Precision.HIGHEST)  102 us
    ppermute x18, starting transfers between devices, passed_along(): lax.ppermute(value, axis, [(source, source + steps) for source in range(i...  36 us
    dot_general x32, matrix products, one_group(): jnp.einsum('ct,ctj->cj', vals, table, precision=lax.Precision.HIGHEST)  25.5 us
    all_to_all x1, waiting for transfers between devices, sent_and_summed(): lax.all_to_all(in_blocks(value, dim, devices), axis, 0, 0, tiled=True)  6.08 us
  transfers between devices with their start and end apart: 19, of which 19 were waited for; matrix products, arithmetic and copies ran while one was open for 0% of the time, Pallas kernels for 0%

commit v1 on v0

v1 whole, which is shorter than its diff:
```python
import functools

import jax
import jax.numpy as jnp
from jax import lax
from jax.experimental import pallas as pl
from jax.experimental.pallas import tpu as pltpu
from jax.sharding import PartitionSpec as P

SUBSTEPS = 3

time_step = 0.5

EXTRA = 8
STORAGE, KAPPA, MASK, FORCING = 0, 1, 2, 3


def vmem():
    return pl.BlockSpec(memory_space=pltpu.VMEM)


def smem():
    return pl.BlockSpec(memory_space=pltpu.SMEM)


def runoff_kernel(water_ref, frac_ref, cell_ref, out_ref):
    rows, tiles = water_ref.shape[1:]
    half = 128
    lanes = lax.broadcasted_iota(jnp.int32, (half, tiles), 0).astype(jnp.float32).astype(jnp.bfloat16)
    one = jnp.ones((half, tiles), jnp.bfloat16)
    zero = jnp.zeros((half, tiles), jnp.bfloat16)

    def block(index, carry):
        at = pl.ds(pl.multiple_of(index * 8, 8), 8)
        value = water_ref[0, at, :] * frac_ref[0, at, :]
        cell = cell_ref[0, at, :]
        upper = cell >= half
        within = jnp.where(upper, cell - half, cell).astype(jnp.float32)
        first = value.astype(jnp.bfloat16).astype(jnp.float32)
        rest = value - first
        second = rest.astype(jnp.bfloat16).astype(jnp.float32)
        third = rest - second
        parts = []
        for piece in (first, second, third):
            parts.append(jnp.where(upper, 0.0, piece))
            parts.append(jnp.where(upper, piece, 0.0))
        outs = []
        for row in range(8):
            left = jnp.concatenate([part[row : row + 1] for part in parts] + [jnp.zeros((2, tiles), jnp.float32)], axis=0)
            owner = jnp.broadcast_to(within[row : row + 1], (half, tiles)).astype(jnp.bfloat16)
            table = jnp.where(owner == lanes, one, zero)
            sums = lax.dot_general(
                left.astype(jnp.bfloat16), table, (((1,), (1,)), ((), ())), preferred_element_type=jnp.float32
            )
            outs.append(jnp.concatenate([sums[0:1] + sums[2:3] + sums[4:5], sums[1:2] + sums[3:4] + sums[5:6]], axis=1))
        out_ref[at, :] = jnp.concatenate(outs, axis=0)
        return carry

    lax.fori_loop(0, rows // 8, block, 0)


def pack_kernel(links_ref, inverse_ref, storage_ref, kappa_ref, mask_ref, pieces_ref, packed_ref, order_ref, small_ref):
    count, rows = links_ref.shape[0], storage_ref.shape[1]
    width = storage_ref.shape[2]
    position = lax.axis_index("basin")

    def back(turn, chains):
        at = count - 1 - turn
        return tuple(links_ref[at, chain] for chain in chains)

    chains = lax.fori_loop(0, count - 1 - position, back, tuple(jnp.int32(q) for q in range(rows)))
    forcing = time_step * jnp.sum(pieces_ref[...], axis=0)
    small_ref[STORAGE] = storage_ref[0]
    small_ref[KAPPA] = kappa_ref[0]
    small_ref[MASK] = mask_ref[0].astype(jnp.float32)
    small_ref[FORCING] = forcing
    tail = jnp.zeros((EXTRA - 4, width), jnp.float32)
    for q in range(rows):
        chain = chains[q]
        packed_ref[q, 0:width, :] = inverse_ref[0, chain]
        lines = [small_ref[kind, pl.ds(chain, 1), :] for kind in range(4)]
        packed_ref[q, width : width + EXTRA, :] = jnp.concatenate(lines + [tail], axis=0)
        order_ref[q : q + 1, :] = jnp.full((1, 128), chain, jnp.int32)


def route_kernel(held_ref, out_ref):
    count = held_ref.shape[0]
    width = held_ref.shape[2]
    half = 128
    diagonal = lax.broadcasted_iota(jnp.int32, (half, half), 0) == lax.broadcasted_iota(jnp.int32, (half, half), 1)

    def turned(column):
        parts = []
        for piece in range(width // half):
            spread = jnp.where(diagonal, column[piece * half : (piece + 1) * half], 0.0)
            parts.append(jnp.sum(spread, axis=0, keepdims=True))
        return jnp.concatenate(parts, axis=1)

    def turn(t, carry):
        levels, flows = carry
        new_levels, new_flows = [], []
        for s in range(SUBSTEPS):
            p = jnp.clip(t - s, 0, count - 1)
            active = jnp.where((t >= s) & (t - s < count), 1.0, 0.0)
            line = lambda kind: held_ref[p, pl.ds(width + kind, 1), :]
            level = line(STORAGE) if s == 0 else levels[s - 1]
            vector = level + line(FORCING) + flows[s]
            column = jnp.sum(held_ref[p, 0:width, :] * vector, axis=1, keepdims=True)
            wet = active * line(MASK) * turned(column)
            flow = line(KAPPA) * wet
            new_levels.append(wet - flow)
            new_flows.append(flow)
        last = jnp.clip(t - (SUBSTEPS - 1), 0, count - 1)
        out_ref[last] = jnp.concatenate([new_levels[-1], new_flows[-1]], axis=0)
        return tuple(new_levels), tuple(new_flows)

    empty = tuple(jnp.zeros((1, width), jnp.float32) for _ in range(SUBSTEPS))
    lax.fori_loop(0, count + SUBSTEPS - 1, turn, (empty, empty))


def unpack_kernel(order_ref, result_ref, level_ref, discharge_ref):
    rows, _, width = result_ref.shape
    chain = lax.broadcasted_iota(jnp.int32, (rows, width), 0)
    level = jnp.zeros((rows, width), jnp.float32)
    discharge = jnp.zeros((rows, width), jnp.float32)
    for q in range(rows):
        mine = chain == order_ref[q : q + 1, 0:1]
        level = jnp.where(mine, result_ref[q, 0:1, :], level)
        discharge = jnp.where(mine, result_ref[q, 1:2, :], discharge)
    level_ref[0] = level
    discharge_ref[0] = discharge


def local(tile_water, tile_frac, tile_cell, storage, kappa, inverse, cell_mask, upstream):
    rows, width = storage.shape[1:]
    positions = lax.axis_size("basin")
    groups = lax.axis_size("tile")
    f32 = jnp.float32
    params = lambda mib: pltpu.CompilerParams(vmem_limit_bytes=mib << 20)

    wide = jnp.pad(upstream, ((0, 0), (0, 128 - rows)))
    links = lax.all_to_all(jnp.broadcast_to(wide, (positions, 128)), "basin", 0, 0, tiled=True)

    partial = pl.pallas_call(
        runoff_kernel,
        out_shape=jax.ShapeDtypeStruct((rows * groups, width), f32),
        in_specs=[vmem()] * 3,
        out_specs=vmem(),
        compiler_params=params(16),
        name="runoff",
    )(tile_water, tile_frac, tile_cell)
    pieces = lax.all_to_all(partial.reshape(groups, rows, width), "tile", 0, 0, tiled=True)

    packed, order = pl.pallas_call(
        pack_kernel,
        out_shape=(
            jax.ShapeDtypeStruct((rows, width + EXTRA, width), f32),
            jax.ShapeDtypeStruct((rows, 128), jnp.int32),
        ),
        in_specs=[smem()] + [vmem()] * 5,
        out_specs=(vmem(), vmem()),
        scratch_shapes=[pltpu.VMEM((4, rows, width), f32)],
        compiler_params=params(16),
        name="pack",
    )(links, inverse, storage, kappa, cell_mask, pieces)
    held = lax.all_to_all(packed, "basin", 0, 0, tiled=True)

    routed = pl.pallas_call(
        route_kernel,
        out_shape=jax.ShapeDtypeStruct((positions, 2, width), f32),
        in_specs=[vmem()],
        out_specs=vmem(),
        compiler_params=params(16),
        name="route",
    )(held)
    result = lax.all_to_all(routed, "basin", 0, 0, tiled=True)

    return pl.pallas_call(
        unpack_kernel,
        out_shape=(jax.ShapeDtypeStruct((1, rows, width), f32), jax.ShapeDtypeStruct((1, rows, width), f32)),
        in_specs=[vmem()] * 2,
        out_specs=(vmem(), vmem()),
        compiler_params=params(4),
        name="unpack",
    )(order, result)


def solution(mesh):
    placed = (
        P("basin", None, "tile"),
        P("basin", None, "tile"),
        P("basin", None, "tile"),
        P("basin", "tile", None),
        P("basin", "tile", None),
        P("basin", "tile", None, None),
        P("basin", "tile", None),
        P("basin", "tile"),
    )
    return jax.shard_map(
        local,
        mesh=mesh,
        in_specs=placed,
        out_specs=(P("basin", "tile", None), P("basin", "tile", None)),
        check_vma=False,
    )
```

time: 289 us -> 110 us (0.38)
  matrix products: 131 us -> 0 us
  waiting for transfers between devices: 109 us -> 0.01 us
  blocking collectives: 0 us -> 79.4 us
  starting transfers between devices: 41.4 us -> 7.39 us
  Pallas kernels: 0 us -> 12 us
  local copies, waits for them, and re-layouts: 2.9 us -> 8.45 us
    dot_general x68 -> x0, matrix products: 131 us -> none  [the longest x18 102 us: update(): jnp.einsum('cjk,ck->cj', matrices, vector, precision=lax.Precision.HIGHEST)]
    ppermute x18 -> x0, waiting for transfers between devices: 103 us -> none  [passed_along(): lax.ppermute(value, axis, [(source, source + steps) for source in range(i...]
    all_to_all x0 -> x3, blocking collectives: none -> 79.4 us  [the longest x1 57.2 us: local(): held = lax.all_to_all(packed, 'basin', 0, 0, tiled=True)]
    ppermute x18 -> x0, starting transfers between devices: 36 us -> none  [passed_along(): lax.ppermute(value, axis, [(source, source + steps) for source in range(i...]
    pallas_call x0 -> x4, Pallas kernels: none -> 12 us  [the longest x1 6.35 us: local(): pl.pallas_call(runoff_kernel, out_shape=jax.ShapeDtypeStruct((rows * grou...]
    unnamed x12 -> x14, local copies, waits for them, and re-layouts: 0.62 us -> 7.18 us
    all_to_all x1, waiting for transfers between devices: 6.08 us -> 0.01 us  [local(): lax.all_to_all(jnp.broadcast_to(wide, (positions, 128)), 'basin', 0, 0, t...]
  transfers between devices with their start and end apart: 19 -> 1, of which waited for: 19 -> 0; matrix products, arithmetic and copies ran while one was open for 0% -> 0% of each run, Pallas kernels for 0% -> 6%
where the time goes in v1:
time: 110 us; the launch traced here: 108 us
  blocking collectives  79.4 us (72%)
  Pallas kernels  12 us (11%)
  local copies, waits for them, and re-layouts  8.45 us (8%)
  starting transfers between devices  7.39 us (7%)
    all_to_all x1, blocking collectives, local(): held = lax.all_to_all(packed, 'basin', 0, 0, tiled=True)  57.2 us
    all_to_all x1, blocking collectives, local(): lax.all_to_all(partial.reshape(groups, rows, width), 'tile', 0, 0, tiled=...  11.2 us
    all_to_all x1, blocking collectives, local(): result = lax.all_to_all(routed, 'basin', 0, 0, tiled=True)  11 us
    all_to_all x1, starting transfers between devices, local(): lax.all_to_all(jnp.broadcast_to(wide, (positions, 128)), 'basin', 0, 0, t...  7.39 us
    unnamed x14, local copies, waits for them, and re-layouts  7.18 us
    pallas_call x1, Pallas kernels, local(): pl.pallas_call(runoff_kernel, out_shape=jax.ShapeDtypeStruct((rows * grou...  6.35 us
    pallas_call x1, Pallas kernels, local(): pl.pallas_call(route_kernel, out_shape=jax.ShapeDtypeStruct((positions, 2...  3.53 us
  transfers between devices with their start and end apart: 1, of which 0 were waited for; matrix products, arithmetic and copies ran while one was open for 0% of the time, Pallas kernels for 6%

profile of v1, /device:TPU:8, one launch (start us, length us, event | category | flops | bytes accessed | tf_op | source)
XLA Modules:
  0.0 107.9 jit_solution(17936121839059543389)
XLA Ops:
  0.6 0.7 pad_bitcast_fusion
  1.3 0.6 broadcast_in_dim.2
  1.9 7.4 %all-to-all-start = ((s32[16,1,128]{2,1,0:T(1,128)}), s32[16,1,128]{2,1,0:T(1,128)S(1)}, u32[]{:S(2)}, u32[]{:S(2)}) async-start(s32[16,1,128]{2,1,0:T(1,128)} %broadcast_in_dim.2), calls=%async_computation | async-start | bytes 16384 | tf_op jit(solution)/shard_map/all_to_all | solution.py:142
  9.3 0.0 copy-start.1
  9.3 0.9 copy-done.1
  10.2 0.0 copy-start.2
  10.2 0.9 copy-done.2
  11.2 0.0 copy-start.3
  11.2 0.9 copy-done.3
  12.1 6.3 %runoff.1 = f32[128,256]{1,0:T(8,128)S(1)} custom-call(f32[1,128,512]{2,1,0:T(8,128)S(1)} %copy-done.1, f32[1,128,512]{2,1,0:T(8,128)S(1)} %copy-done.2, s32[1,128,512]{2,1,0:T(8,128)S(1)} %copy-done.3), custom_call_target="tpu_custom_call" | custom-call | tf_op jit(solution)/shard_map/runoff/pallas_call | solution.py:144
  18.5 0.0 all-to-all-done
  18.5 11.2 %all_to_all.23.pieces_ref = f32[8,16,256]{2,1,0:T(8,128)S(1)} all-to-all(f32[8,16,256]{2,1,0:T(8,128)S(1)} %bitcast.4), channel_id=1, replica_groups=mesh['basin'=16,'tile'=8] {'tile'}, dimensions={0} | all-to-all | bytes 262144 | tf_op jit(solution)/shard_map/all_to_all | solution.py:152
  29.7 0.0 copy-start
  29.7 2.2 %copy-done = f32[1,16,256,256]{3,2,1,0:T(8,128)S(1)} copy-done((f32[1,16,256,256]{3,2,1,0:T(8,128)S(1)}, f32[1,16,256,256]{3,2,1,0:T(8,128)}, u32[]{:S(2)}) %copy-start) | copy-done | bytes 4194328
  31.9 0.0 copy-start.4
  31.9 0.7 copy-done.4
  32.6 0.0 copy-start.5
  32.6 0.7 copy-done.5
  33.3 0.0 copy-start.6
  33.3 0.7 copy-done.6
  34.1 1.4 %pack.1 = (f32[16,264,256]{2,1,0:T(8,128)S(1)}, s32[16,128]{1,0:T(8,128)S(1)}) custom-call(s32[16,128]{1,0:T(8,128)S(1)} %bitcast.5, f32[1,16,256,256]{3,2,1,0:T(8,128)S(1)} %copy-done, f32[1,16,256]{2,1,0:T(8,128)S(1)} %copy-done.4, f32[1,16,256]{2,1,0:T(8,128)S(1)} %copy-done.5, s32[1,16,256]{2,1,0:T(8,128)S(1)} %copy-done.6, ...), custom_call_target="tpu_custom_call" | custom-call | tf_op jit(solution)/shard_map/pack/pallas_call | solution.py:154
  35.5 57.2 %all_to_all.24.held_ref = f32[16,264,256]{2,1,0:T(8,128)S(1)} all-to-all(f32[16,264,256]{2,1,0:T(8,128)S(1)} %get-tuple-element.5), channel_id=1, replica_groups=mesh['basin'=16,'tile'=8] {'basin'}, dimensions={0} | all-to-all | bytes 8650752 | tf_op jit(solution)/shard_map/all_to_all | solution.py:166
  92.7 3.5 %route.1 = f32[16,2,256]{2,1,0:T(2,128)S(1)} custom-call(f32[16,264,256]{2,1,0:T(8,128)S(1)} %all_to_all.24.held_ref), custom_call_target="tpu_custom_call" | custom-call | tf_op jit(solution)/shard_map/route/pallas_call | solution.py:168
  96.2 11.0 %all_to_all.25.result_ref = f32[16,2,256]{2,1,0:T(2,128)S(1)} all-to-all(f32[16,2,256]{2,1,0:T(2,128)S(1)} %route.1), channel_id=1, replica_groups=mesh['basin'=16,'tile'=8] {'basin'}, dimensions={0} | all-to-all | bytes 65536 | tf_op jit(solution)/shard_map/all_to_all | solution.py:176
  107.2 0.7 unpack.1
Async XLA Ops:
  1.9 16.6 %all-to-all-start = ((s32[16,1,128]{2,1,0:T(1,128)}), s32[16,1,128]{2,1,0:T(1,128)S(1)}, u32[]{:S(2)}, u32[]{:S(2)}) async-start(s32[16,1,128]{2,1,0:T(1,128)} %broadcast_in_dim.2), calls=%async_computation | async-start | bytes 16384 | tf_op jit(solution)/shard_map/all_to_all | solution.py:142
  9.3 0.9 copy-start.1
  10.2 0.9 copy-start.2
  11.2 0.9 copy-start.3
  29.7 2.2 %copy-start = (f32[1,16,256,256]{3,2,1,0:T(8,128)S(1)}, f32[1,16,256,256]{3,2,1,0:T(8,128)}, u32[]{:S(2)}) copy-start(f32[1,16,256,256]{3,2,1,0:T(8,128)} %inverse_ref.1) | copy-start | bytes 12582916
  31.9 0.7 copy-start.4
  32.6 0.7 copy-start.5
  33.3 0.7 copy-start.6
